TPU v7x, 1024 devices: a whole 8x8x8 slice. The times are simulated.
1024 devices in a mesh: row: 32 (over y, x_lo), col: 16 (over z, x_hi), layer: 2 (over core).
Axes of the slice: x: 8 (x_hi: 2, x_lo: 4; x = x_hi * 4 + x_lo), y: 8, z: 8, core: 2. Of those that a mesh axis runs over, the one named last changes fastest.
Arguments:
- hamiltonian: bfloat16 [32768, 32768], P('row', 'col'), as said below
- start_vectors: bfloat16 [256, 32768], P('row', ('col', 'layer')), may hold values from -6 to 6
- cut_low: float32 [1], replicated, may hold values from -1.6 to -1.2
- cut_high: float32 [1], replicated, may hold values from 2 to 2.4
Outputs:
- filtered: bfloat16 [256, 32768], P('row', ('col', 'layer'))
Inputs may be any that keep to these rules, and one draw needn't show every extreme that they name: hamiltonian is exactly symmetric.
All inputs are finite; a program needn't handle non-finite values.
Results may differ from a plain program's by a relative error of at most 0.009.
Values may be sent and summed in bfloat16 or wider, within the bound.
A program may use at most 32 MiB of HBM per device.

v0:
```python
import jax
import jax.numpy as jnp
from jax import lax
from jax.sharding import PartitionSpec as P


def joined_along(blocks, dim):
    shape = list(blocks.shape[1:])
    shape[dim] *= blocks.shape[0]
    return jnp.moveaxis(blocks, 0, dim).reshape(shape)


def copy_for_each(shard, axis):
    copies = jnp.broadcast_to(shard, (lax.axis_size(axis), *shard.shape))
    return lax.all_to_all(copies, axis, split_axis=0, concat_axis=0, tiled=True)


def gathered_copies(shard, axis, dim):
    return joined_along(copy_for_each(shard, axis), dim)


def cut_along(shard, dim, count):
    before, after = (shard.shape[:dim], shard.shape[dim + 1 :])
    return jnp.moveaxis(shard.reshape(*before, count, -1, *after), dim, 0)


def sum_at_owner(shard, axis, dim):
    blocks = cut_along(shard, dim, lax.axis_size(axis))
    arrived = lax.all_to_all(blocks, axis, split_axis=0, concat_axis=0, tiled=True)
    return arrived.sum(axis=0)


def make_shifted(block, first_row, first_col, centre, half_width):
    row_count, col_count = block.shape
    row_ids = lax.broadcasted_iota(jnp.int32, (row_count, col_count), 0) + first_row
    col_ids = lax.broadcasted_iota(jnp.int32, (row_count, col_count), 1) + first_col
    diagonal_mask = (row_ids == col_ids).astype(jnp.float32)
    return ((block.astype(jnp.float32) - centre * diagonal_mask) / half_width).astype(jnp.bfloat16)


def recurrence(begin, by_columns, by_rows):
    first = by_columns(begin).astype(jnp.bfloat16)
    second = (2.0 * by_rows(first) - begin.astype(jnp.float32)).astype(jnp.bfloat16)
    third = (2.0 * by_columns(second) - first.astype(jnp.float32)).astype(jnp.bfloat16)
    return (2.0 * by_rows(third) - second.astype(jnp.float32)).astype(jnp.bfloat16)


def local(hamiltonian, start_vectors, cut_low, cut_high):
    centre = (cut_low[0] + cut_high[0]) * 0.5
    half_width = (cut_high[0] - cut_low[0]) * 0.5
    row_count = hamiltonian.shape[0]
    first_row = lax.axis_index("row") * row_count
    width = hamiltonian.shape[1]
    whole = make_shifted(hamiltonian, first_row, lax.axis_index("col") * width, centre, half_width)

    def left_whole(panel):
        return lax.dot_general(
            panel, whole, (((1,), (1,)), ((), ())), preferred_element_type=jnp.float32
        )

    def right_whole(panel):
        return jnp.dot(panel, whole, preferred_element_type=jnp.float32)

    def by_columns(vectors):
        partial_value = left_whole(gathered_copies(vectors, "row", 0))
        return sum_at_owner(partial_value, "col", 0)

    def by_rows(vectors):
        partial_value = right_whole(gathered_copies(vectors, "col", 0))
        return sum_at_owner(partial_value, "row", 0)

    begin = lax.all_to_all(start_vectors, "layer", split_axis=0, concat_axis=1, tiled=True)
    result = recurrence(begin, by_columns, by_rows)
    return lax.all_to_all(result, "layer", split_axis=1, concat_axis=0, tiled=True)


def solution(mesh):
    return jax.shard_map(
        local,
        mesh=mesh,
        in_specs=(P("row", "col"), P("row", ("col", "layer")), P(), P()),
        out_specs=P("row", ("col", "layer")),
        check_vma=False,
    )
```

profile of v0, /device:TPU:1, one launch (start us, length us, event | category | flops | bytes accessed | tf_op | source)
XLA Modules:
  0.0 243.9 jit_solution(6693280422954126476)
XLA Ops:
  0.0 0.7 all_to_all.50
  0.7 17.5 %all_to_all.75 = bf16[2,4,1024]{2,1,0:T(4,128)(2,1)S(1)} all-to-all(bf16[2,4,1024]{2,1,0:T(4,128)(2,1)S(1)} %all_to_all.50), channel_id=1, replica_groups=mesh['row'=32,'col'=16,'layer'=2] {'layer'}, dimensions={0} | all-to-all | bytes 32768 | tf_op jit(solution)/shard_map/all_to_all | solution.py:72
  18.2 1.0 broadcast_in_dim.12
  19.3 3.9 %all-to-all-start.1 = ((bf16[32,4,2048]{2,1,0:T(4,128)(2,1)}), bf16[32,4,2048]{2,1,0:T(4,128)(2,1)S(1)}, u32[]{:S(2)}, u32[]{:S(2)}) async-start(bf16[32,4,2048]{2,1,0:T(4,128)(2,1)} %broadcast_in_dim.12), calls=%async_computation.1 | async-start | bytes 1048576 | tf_op jit(solution)/shard_map/all_to_all | solution.py:15
  24.5 4.7 %divide_convert_fusion = bf16[1024,2048]{1,0:T(8,128)(2,1)} fusion(bf16[1024,2048]{1,0:T(8,128)(2,1)} %param.4, f32[]{:T(128)} %bitcast.1, f32[]{:T(128)} %bitcast, s32[2048]{0:T(1024)S(1)} %iota_add_fusion, s32[1024]{0:T(1024)S(1)} %iota_add_fusion.1), kind=kLoop, calls=%fused_computation | loop fusion | flops 12582912 | bytes 8400904 | tf_op jit(solution)/shard_map/convert_element_type | solution.py:38
  29.2 9.6 %all-to-all-done.1 = bf16[32,4,2048]{2,1,0:T(4,128)(2,1)S(1)} async-done(((bf16[32,4,2048]{2,1,0:T(4,128)(2,1)}), bf16[32,4,2048]{2,1,0:T(4,128)(2,1)S(1)}, u32[]{:S(2)}, u32[]{:S(2)}) %all-to-all-start.1) | async-done | bytes 524320 | tf_op jit(solution)/shard_map/all_to_all | solution.py:15
  38.8 0.1 reshape.36
  38.9 3.7 %convolution_bitcast_fusion = f32[16,8,1024]{2,1,0:T(8,128)S(1)} fusion(bf16[1024,2048]{1,0:T(8,128)(2,1)} %divide_convert_fusion, bf16[128,2048]{1,0:T(8,128)(2,1)S(1)} %reshape.36), kind=kOutput, calls=%fused_computation.7 | convolution fusion | flops 536870912 | bytes 5242880 | tf_op jit(solution)/shard_map/dot_general | solution.py:57
  42.6 26.2 %all_to_all.76 = f32[16,8,1024]{2,1,0:T(8,128)S(1)} all-to-all(f32[16,8,1024]{2,1,0:T(8,128)S(1)} %convolution_bitcast_fusion), channel_id=1, replica_groups=mesh['row'=32,'col'=16,'layer'=2] {'col'}, dimensions={0} | all-to-all | bytes 1048576 | tf_op jit(solution)/shard_map/all_to_all | solution.py:29
  68.9 22.7 %all_to_all.77 = bf16[16,8,1024]{2,1,0:T(8,128)(2,1)S(1)} all-to-all(bf16[16,8,1024]{2,1,0:T(8,128)(2,1)S(1)} %broadcast_in_dim.13), channel_id=1, replica_groups=mesh['row'=32,'col'=16,'layer'=2] {'col'}, dimensions={0} | all-to-all | bytes 524288 | tf_op jit(solution)/shard_map/all_to_all | solution.py:15
  91.6 0.1 dot_general.22
  91.7 2.9 %fusion.4 = f32[32,4,2048]{2,0,1:T(8,128)S(1)} fusion(bf16[1024,2048]{1,0:T(8,128)(2,1)} %divide_convert_fusion, bf16[32,4,1024]{2,1,0:T(4,128)(2,1)S(1)} %dot_general.22), kind=kOutput, calls=%fused_computation.5 | convolution fusion | flops 536870912 | bytes 5505024 | tf_op jit(solution)/shard_map/dot_general | solution.py:62
  94.7 0.7 copy.8
  95.4 35.1 %all_to_all.78 = f32[32,4,2048]{2,1,0:T(4,128)S(1)} all-to-all(f32[32,4,2048]{2,1,0:T(4,128)S(1)} %copy.8), channel_id=1, replica_groups=mesh['row'=32,'col'=16,'layer'=2] {'row'}, dimensions={0} | all-to-all | bytes 2097152 | tf_op jit(solution)/shard_map/all_to_all | solution.py:29
  130.5 0.2 reduce_sum.37
  130.7 0.2 broadcast_in_dim.14
  130.9 21.3 %all_to_all.79 = bf16[32,4,2048]{2,1,0:T(4,128)(2,1)S(1)} all-to-all(bf16[32,4,2048]{2,1,0:T(4,128)(2,1)S(1)} %broadcast_in_dim.14), channel_id=1, replica_groups=mesh['row'=32,'col'=16,'layer'=2] {'row'}, dimensions={0} | all-to-all | bytes 1048576 | tf_op jit(solution)/shard_map/all_to_all | solution.py:15
  152.2 0.1 dot_general.24
  152.3 3.7 %fusion.2 = f32[16,8,1024]{2,1,0:T(8,128)S(1)} fusion(bf16[16,8,2048]{2,1,0:T(8,128)(2,1)S(1)} %dot_general.24, bf16[1024,2048]{1,0:T(8,128)(2,1)} %divide_convert_fusion), kind=kOutput, calls=%fused_computation.3 | convolution fusion | flops 536870912 | bytes 5242880 | tf_op jit(solution)/shard_map/dot_general | solution.py:57
  156.0 19.5 %all_to_all.80 = f32[16,8,1024]{2,1,0:T(8,128)S(1)} all-to-all(f32[16,8,1024]{2,1,0:T(8,128)S(1)} %fusion.2), channel_id=1, replica_groups=mesh['row'=32,'col'=16,'layer'=2] {'col'}, dimensions={0} | all-to-all | bytes 1048576 | tf_op jit(solution)/shard_map/all_to_all | solution.py:29
  175.5 22.9 %all_to_all.81 = bf16[16,8,1024]{2,1,0:T(8,128)(2,1)S(1)} all-to-all(bf16[16,8,1024]{2,1,0:T(8,128)(2,1)S(1)} %broadcast_in_dim.15), channel_id=1, replica_groups=mesh['row'=32,'col'=16,'layer'=2] {'col'}, dimensions={0} | all-to-all | bytes 524288 | tf_op jit(solution)/shard_map/all_to_all | solution.py:15
  198.5 0.1 dot_general.26
  198.6 2.9 %fusion = f32[32,4,2048]{2,0,1:T(8,128)S(1)} fusion(bf16[1024,2048]{1,0:T(8,128)(2,1)} %divide_convert_fusion, bf16[32,4,1024]{2,1,0:T(4,128)(2,1)S(1)} %dot_general.26), kind=kOutput, calls=%fused_computation.1 | convolution fusion | flops 536870912 | bytes 5505024 | tf_op jit(solution)/shard_map/dot_general | solution.py:62
  201.5 0.7 copy.10
  202.2 35.4 %all_to_all.82 = f32[32,4,2048]{2,1,0:T(4,128)S(1)} all-to-all(f32[32,4,2048]{2,1,0:T(4,128)S(1)} %copy.10), channel_id=1, replica_groups=mesh['row'=32,'col'=16,'layer'=2] {'row'}, dimensions={0} | all-to-all | bytes 2097152 | tf_op jit(solution)/shard_map/all_to_all | solution.py:29
  237.6 0.2 reduce_sum.39
  237.8 5.5 %all_to_all.83 = bf16[4,2,1024]{2,0,1:T(4,128)(2,1)S(1)} all-to-all(bf16[4,2,1024]{2,0,1:T(4,128)(2,1)S(1)} %subtract_convert_fusion), channel_id=1, replica_groups=mesh['row'=32,'col'=16,'layer'=2] {'layer'}, dimensions={1} | all-to-all | bytes 32768 | tf_op jit(solution)/shard_map/all_to_all | solution.py:74
  243.3 0.6 all_to_all.64
  (10 shorter events, 0.2 us)
Async XLA Ops:
  19.3 19.5 %all-to-all-start.1 = ((bf16[32,4,2048]{2,1,0:T(4,128)(2,1)}), bf16[32,4,2048]{2,1,0:T(4,128)(2,1)S(1)}, u32[]{:S(2)}, u32[]{:S(2)}) async-start(bf16[32,4,2048]{2,1,0:T(4,128)(2,1)} %broadcast_in_dim.12), calls=%async_computation.1 | async-start | bytes 1048576 | tf_op jit(solution)/shard_map/all_to_all | solution.py:15
where the time goes:
time: 245 us; the launch traced here: 244 us
  blocking collectives  206 us (84%)
  matrix products  13.3 us (5%)
  waiting for transfers between devices  9.61 us (4%)
  other arithmetic  5.15 us (2%)
  local copies, waits for them, and re-layouts  4.45 us (2%)
  starting transfers between devices  3.89 us (2%)
    all_to_all x4, blocking collectives, sum_at_owner(): lax.all_to_all(blocks, axis, split_axis=0, concat_axis=0, tiled=True)  116 us
    all_to_all x3, blocking collectives, copy_for_each(): return lax.all_to_all(copies, axis, split_axis=0, concat_axis=0, tiled=True)  66.9 us
    all_to_all x1, blocking collectives, local(): lax.all_to_all(start_vectors, 'layer', split_axis=0, concat_axis=1, tiled...  17.5 us
    all_to_all x1, waiting for transfers between devices, copy_for_each(): return lax.all_to_all(copies, axis, split_axis=0, concat_axis=0, tiled=True)  9.61 us
    dot_general x2, matrix products, left_whole(): lax.dot_general(panel, whole, (((1,), (1,)), ((), ())), preferred_element...  7.38 us
    dot_general x2, matrix products, right_whole(): return jnp.dot(panel, whole, preferred_element_type=jnp.float32)  5.89 us
    all_to_all x1, blocking collectives, local(): lax.all_to_all(result, 'layer', split_axis=1, concat_axis=0, tiled=True)  5.47 us
  transfers between devices with their start and end apart: 1, of which 1 were waited for; matrix products, arithmetic and copies ran while one was open for 2% of the time, Pallas kernels for 0%

commit v1 on v0

v1 whole, which is shorter than its diff:
```python
import functools

import jax
import jax.numpy as jnp
from jax import lax
from jax.experimental import pallas as pl
from jax.experimental.pallas import tpu as pltpu
from jax.sharding import PartitionSpec as P

MESH = pl.DeviceIdType.MESH
F32, BF16 = jnp.float32, jnp.bfloat16
CHAINS = 2


def ds(start, size):
    return pl.ds(pl.multiple_of(start, size), size)


def kernel(low_ref, high_ref, h_hbm, start_ref, out_ref,
           h, raw, panel0, colsend, colrecv, colsum, pairsend, pairrecv, panel1,
           rowsend, rowrecv, panel2, lastsend, lastrecv,
           h_sem, s_start, r_start, s_own, r_own, s_cut, r_cut, s_pair, r_pair, s_all, r_all,
           s_row, r_row, s_full, r_full, s_last, r_last, s_lown, r_lown):
    r, c, l = lax.axis_index("row"), lax.axis_index("col"), lax.axis_index("layer")
    y, z, xh = r // 4, c // 2, c % 2
    mine = (y + r % 4) % 4
    my_core, my_k = mine // CHAINS, mine % CHAINS

    loads = [
        pltpu.make_async_copy(h_hbm.at[pl.ds(256 * i, 256)], h.at[pl.ds(256 * i, 256)], h_sem.at[i])
        for i in range(4)
    ]
    for load in loads:
        load.start()

    def send(src, dst, s_sem, r_sem, row, col, layer):
        pltpu.make_async_remote_copy(
            src_ref=src, dst_ref=dst, send_sem=s_sem, recv_sem=r_sem,
            device_id=(row, col, layer), device_id_type=MESH,
        ).start()

    def wait(ref, sem):
        pltpu.make_async_copy(ref, ref, sem).wait()

    def each(n, body):
        def step(i, carry):
            body(i)
            return carry

        lax.fori_loop(0, n, step, 0)

    barrier = pltpu.get_barrier_semaphore()

    def greet(row, col, layer):
        pl.semaphore_signal(barrier, inc=1, device_id=(row, col, layer), device_id_type=MESH)

    def greet_row(i):
        greet((r + i + 1) % 32, c, l)
        greet((r + i + 1) % 32, c, 1 - l)

    each(31, greet_row)
    greet(r, c, 1 - l)
    each(7, lambda i: greet(r, 2 * ((z + i + 1) % 8) + xh, l))
    greet(r, 2 * z + 1 - xh, l)
    pl.semaphore_wait(barrier, 71)

    landing = raw.at[my_k, y, :, ds(l * 1024, 1024)]
    each(31, lambda i: send(start_ref, landing, s_start, r_start.at[my_k], (r + i + 1) % 32, c, my_core))

    @pl.when(l == my_core)
    def _():
        raw[my_k, y, :, ds(l * 1024, 1024)] = start_ref[...]

    @pl.when(l != my_core)
    def _():
        send(start_ref, landing, s_own, r_own, r, c, my_core)

    low, high = low_ref[0], high_ref[0]
    centre = (low + high) * 0.5
    half_width = (high - low) * 0.5
    scale = 1.0 / half_width
    diag = [
        jnp.where((r // 2 == c) & (r % 2 == half), centre, 0.0) for half in range(2)
    ]

    for load in loads:
        load.wait()

    def take_start(k):
        own = 2 * l + k == mine

        @pl.when(own)
        def _():
            wait(raw.at[k, pl.ds(0, 7)], r_start.at[k])

            @pl.when(l == my_core)
            def _():
                wait(raw.at[k, y, :, ds((1 - l) * 1024, 1024)], r_own)

        @pl.when(jnp.logical_not(own))
        def _():
            wait(raw.at[k], r_start.at[k])

        for i in range(4):
            pair = jnp.concatenate([raw[k, 2 * i].astype(F32), raw[k, 2 * i + 1].astype(F32)], axis=0)
            panel0[k, 16 * i:16 * i + 16, :] = pair.astype(BF16)

    def by_columns(s, k, panel):
        for n in range(4):
            cols = slice(256 * n, 256 * n + 256)
            value = lax.dot_general(
                panel[k], h[cols, :], (((1,), (1,)), ((), ())), preferred_element_type=F32
            )
            for half in range(2):
                lo = 1024 * half + 256 * n
                value = value - diag[half] * panel[k, :, lo:lo + 256].astype(F32)
            colsend[s, k, :, cols] = value.astype(BF16)

        def to(i):
            other = (z + i + 1) % 8
            send(colsend.at[s, k, ds(16 * (other // 2), 16), ds(512 * (other % 2), 512)],
                 colrecv.at[s, k, z], s_cut.at[s, k], r_cut.at[s, k], r, 2 * other + xh, l)

        each(7, to)
        colrecv[s, k, z] = colsend[s, k, ds(16 * (z // 2), 16), ds(512 * (z % 2), 512)]

    def pair_up(s, k):
        wait(colrecv.at[s, k, pl.ds(0, 7)], r_cut.at[s, k])
        total = colrecv[s, k, 0].astype(F32)
        for i in range(1, 8):
            total = total + colrecv[s, k, i].astype(F32)
        colsum[s, k] = total
        pairsend[s, k] = total.astype(BF16)
        send(pairsend.at[s, k], pairrecv.at[s, k], s_pair.at[s, k], r_pair.at[s, k], r, 2 * z + 1 - xh, l)

    def spread_first(s, k):
        wait(pairrecv.at[s, k], r_pair.at[s, k])
        total = colsum[s, k] + pairrecv[s, k].astype(F32)
        rows, cols = ds(16 * (z // 2), 16), ds(512 * (z % 2), 512)
        if s == 0:
            value = scale * total
        else:
            value = 2.0 * scale * total - panel1[0, k, rows, cols].astype(F32)
        panel1[s, k, rows, cols] = value.astype(BF16)
        piece = panel1.at[s, k, rows, cols]
        each(7, lambda i: send(piece, piece, s_all.at[s, k], r_all.at[s, k], r, 2 * ((z + i + 1) % 8) + xh, l))

    def by_rows(s, k):
        wait(colrecv.at[s, k, pl.ds(0, 7)], r_all.at[s, k])
        own = 2 * l + k == mine
        for n in range(8):
            cols = slice(256 * n, 256 * n + 256)
            lo = (256 * n) % 1024
            value = jnp.dot(panel1[s, k], h[:, cols], preferred_element_type=F32)
            value = value - diag[n // 4] * panel1[s, k, :, lo:lo + 256].astype(F32)
            if s == 0:
                rowsend[k, :, cols] = value.astype(BF16)
            else:
                second = panel2[k, :, cols].astype(F32)
                for i in range(8):
                    rows = slice(8 * i, 8 * i + 8)
                    share = jnp.where(own & (y == i), half_width * 0.5, 0.0)
                    lastsend[k, i, :, cols] = (value[rows] - share * second[rows]).astype(BF16)

    def cut_rows(k):
        def to(i):
            other = (r + i + 1) % 32
            send(rowsend.at[k, ds(16 * (other // 8), 16), ds(256 * (other % 8), 256)],
                 rowrecv.at[k, r], s_row.at[k], r_row.at[k], other, c, l)

        each(31, to)
        rowrecv[k, r] = rowsend[k, ds(16 * (r // 8), 16), ds(256 * (r % 8), 256)]

    def spread_second(k):
        wait(rowrecv.at[k, pl.ds(0, 31)], r_row.at[k])
        total = rowrecv[k, 0].astype(F32)
        for i in range(1, 32):
            total = total + rowrecv[k, i].astype(F32)
        rows, cols = ds(16 * (r // 8), 16), ds(256 * (r % 8), 256)
        value = 2.0 * scale * total - panel0[k, rows, cols].astype(F32)
        panel2[k, rows, cols] = value.astype(BF16)
        piece = panel2.at[k, rows, cols]
        each(31, lambda i: send(piece, piece, s_full.at[k], r_full.at[k], (r + i + 1) % 32, c, l))

    def send_last(k):
        own = 2 * l + k == mine

        def to(i):
            py = (y + i) % 8
            other = 4 * py + (2 * l + k + 8 - py) % 4

            @pl.when(other != r)
            def _():
                for half in range(2):
                    send(lastsend.at[k, py, :, pl.ds(1024 * half, 1024)], lastrecv.at[r],
                         s_last.at[k], r_last, other, c, half)

        each(8, to)

        @pl.when(own)
        def _():
            lastrecv[r] = lastsend[k, y, :, ds(1024 * l, 1024)]
            send(lastsend.at[k, y, :, ds(1024 * (1 - l), 1024)], lastrecv.at[r], s_lown, r_lown, r, c, 1 - l)

    def begin(k):
        take_start(k)
        by_columns(0, k, panel0)

    each(CHAINS, begin)
    each(CHAINS, lambda k: pair_up(0, k))
    each(CHAINS, lambda k: spread_first(0, k))

    def middle(k):
        by_rows(0, k)
        cut_rows(k)

    each(CHAINS, middle)
    each(CHAINS, spread_second)

    def again(k):
        wait(rowrecv.at[k, pl.ds(0, 31)], r_full.at[k])
        by_columns(1, k, panel2)

    each(CHAINS, again)
    each(CHAINS, lambda k: pair_up(1, k))
    each(CHAINS, lambda k: spread_first(1, k))

    def finish(k):
        by_rows(1, k)
        send_last(k)

    each(CHAINS, finish)

    wait(lastrecv.at[pl.ds(0, 31)], r_last)

    @pl.when(l != my_core)
    def _():
        wait(lastrecv.at[31], r_lown)

    total = lastrecv[0].astype(F32)
    for i in range(1, 32):
        total = total + lastrecv[i].astype(F32)
    out_ref[...] = (2.0 * scale * total).astype(BF16)

    wait(lastrecv.at[pl.ds(0, 31)], s_start)

    @pl.when(l != my_core)
    def _():
        wait(start_ref, s_own)

    @pl.when(l == my_core)
    def _():
        wait(lastrecv.at[31], s_lown)

    def drain(k):
        for s in range(2):
            wait(colrecv.at[s, k, pl.ds(0, 7)], s_cut.at[s, k])
            wait(pairsend.at[s, k], s_pair.at[s, k])
            wait(colrecv.at[s, k, pl.ds(0, 7)], s_all.at[s, k])
        wait(rowrecv.at[k, pl.ds(0, 31)], s_row.at[k])
        wait(rowrecv.at[k, pl.ds(0, 31)], s_full.at[k])
        own = 2 * l + k == mine

        @pl.when(own)
        def _():
            wait(lastsend.at[k, pl.ds(0, 7)], s_last.at[k])

        @pl.when(jnp.logical_not(own))
        def _():
            wait(lastsend.at[k], s_last.at[k])

    each(CHAINS, drain)


def local(hamiltonian, start_vectors, cut_low, cut_high):
    vmem, dma = pltpu.VMEM, pltpu.SemaphoreType.DMA
    n = CHAINS
    return pl.pallas_call(
        kernel,
        out_shape=jax.ShapeDtypeStruct(start_vectors.shape, BF16),
        in_specs=[
            pl.BlockSpec(memory_space=pltpu.SMEM),
            pl.BlockSpec(memory_space=pltpu.SMEM),
            pl.BlockSpec(memory_space=pl.ANY),
            pl.BlockSpec(memory_space=pltpu.VMEM),
        ],
        out_specs=pl.BlockSpec(memory_space=pltpu.VMEM),
        scratch_shapes=[
            vmem((1024, 2048), BF16),
            vmem((n, 8, 8, 2048), BF16),
            vmem((n, 64, 2048), BF16),
            vmem((2, n, 64, 1024), BF16),
            vmem((2, n, 8, 16, 512), BF16),
            vmem((2, n, 16, 512), F32),
            vmem((2, n, 16, 512), BF16),
            vmem((2, n, 16, 512), BF16),
            vmem((2, n, 64, 1024), BF16),
            vmem((n, 64, 2048), BF16),
            vmem((n, 32, 16, 256), BF16),
            vmem((n, 64, 2048), BF16),
            vmem((n, 8, 8, 2048), BF16),
            vmem((32, 8, 1024), BF16),
            dma((4,)),
            dma, dma((n,)), dma, dma,
            dma((2, n)), dma((2, n)), dma((2, n)), dma((2, n)), dma((2, n)), dma((2, n)),
            dma((n,)), dma((n,)), dma((n,)), dma((n,)),
            dma((n,)), dma, dma, dma,
        ],
        compiler_params=pltpu.CompilerParams(
            collective_id=0, has_side_effects=True, vmem_limit_bytes=40 * 1024 * 1024
        ),
        name="filter",
    )(cut_low, cut_high, hamiltonian, start_vectors)


def solution(mesh):
    return jax.shard_map(
        local,
        mesh=mesh,
        in_specs=(P("row", "col"), P("row", ("col", "layer")), P(), P()),
        out_specs=P("row", ("col", "layer")),
        check_vma=False,
    )
```

time: 245 us -> 119 us (0.49)
  blocking collectives: 206 us -> 0 us
  Pallas kernels: 0 us -> 113 us
  matrix products: 13.3 us -> 0 us
  waiting for transfers between devices: 9.61 us -> 0 us
  other arithmetic: 5.15 us -> 0 us
  starting transfers between devices: 3.89 us -> 0 us
    all_to_all x9 -> x0, blocking collectives: 206 us -> none  [the longest x4 116 us: sum_at_owner(): lax.all_to_all(blocks, axis, split_axis=0, concat_axis=0, tiled=True)]
    pallas_call x0 -> x1, Pallas kernels: none -> 113 us  [local(): pl.pallas_call(kernel, out_shape=jax.ShapeDtypeStruct(start_vectors.shape...]
    dot_general x4 -> x0, matrix products: 13.3 us -> none  [the longest x2 7.38 us: left_whole(): lax.dot_general(panel, whole, (((1,), (1,)), ((), ())), preferred_element...]
    all_to_all x1 -> x0, waiting for transfers between devices: 9.61 us -> none  [copy_for_each(): return lax.all_to_all(copies, axis, split_axis=0, concat_axis=0, tiled=True)]
    convert_element_type x3 -> x0, other arithmetic: 4.71 us -> none  [the longest x1 4.68 us: make_shifted(): ((block.astype(jnp.float32) - centre * diagonal_mask) / half_width).astyp...]
    all_to_all x1 -> x0, starting transfers between devices: 3.89 us -> none  [copy_for_each(): return lax.all_to_all(copies, axis, split_axis=0, concat_axis=0, tiled=True)]
    unnamed x0 -> x5, local copies, waits for them, and re-layouts: none -> 3.51 us
  transfers between devices with their start and end apart: 1 -> 0, of which waited for: 1 -> 0; matrix products, arithmetic and copies ran while one was open for 2% -> 0% of each run, Pallas kernels for 0% -> 0%
where the time goes in v1:
time: 119 us; the launch traced here: 118 us
  Pallas kernels  113 us (95%)
  local copies, waits for them, and re-layouts  3.51 us (3%)
  between operations  1.31 us (1%)
    pallas_call x1, Pallas kernels, local(): pl.pallas_call(kernel, out_shape=jax.ShapeDtypeStruct(start_vectors.shape...  113 us
    unnamed x5, local copies, waits for them, and re-layouts  3.51 us

profile of v1, /device:TPU:1, one launch (start us, length us, event | category | flops | bytes accessed | tf_op | source)
XLA Modules:
  0.0 117.7 jit_solution(14001938543794014749)
XLA Ops:
  1.3 0.0 copy-start
  1.3 2.2 %copy-done = bf16[1024,2048]{1,0:T(8,128)(2,1)S(1)} copy-done((bf16[1024,2048]{1,0:T(8,128)(2,1)S(1)}, bf16[1024,2048]{1,0:T(8,128)(2,1)}, u32[]{:S(2)}) %copy-start) | copy-done | bytes 4194328
  3.5 0.0 copy-start.1
  3.5 0.7 copy-done.1
  4.2 112.8 %filter.1 = bf16[8,1024]{1,0:T(8,128)(2,1)S(1)} custom-call(f32[1]{0:T(128)S(6)} %copy.6.low_ref, f32[1]{0:T(128)S(6)} %copy.7.high_ref, bf16[1024,2048]{1,0:T(8,128)(2,1)S(1)} %copy-done, bf16[8,1024]{1,0:T(8,128)(2,1)S(1)} %copy-done.1), custom_call_target="tpu_custom_call" | custom-call | tf_op jit(solution)/shard_map/filter/pallas_call | solution.py:278
  117.1 0.6 copy.8
Async XLA Ops:
  1.3 2.2 %copy-start = (bf16[1024,2048]{1,0:T(8,128)(2,1)S(1)}, bf16[1024,2048]{1,0:T(8,128)(2,1)}, u32[]{:S(2)}) copy-start(bf16[1024,2048]{1,0:T(8,128)(2,1)} %h_hbm.1) | copy-start | bytes 12582916
  3.5 0.7 copy-start.1

commit v2 on v1

v2 whole, which is shorter than its diff:
```python
import functools

import jax
import jax.numpy as jnp
from jax import lax
from jax.experimental import pallas as pl
from jax.experimental.pallas import tpu as pltpu
from jax.sharding import PartitionSpec as P

MESH = pl.DeviceIdType.MESH
F32, BF16 = jnp.float32, jnp.bfloat16
CHAINS = 4


def ds(start, size):
    return pl.ds(pl.multiple_of(start, size), size)


def kernel(low_ref, high_ref, h_hbm, start_hbm, out_ref,
           h, start, startsend, raw, panel0, colsend, colrecv, colsum, pairsend, pairrecv, panel1,
           rowsend, rowrecv, panel2, lastsend, lastrecv,
           h_sem, start_sem, s_start, r_start, s_own, r_own, s_cut, r_cut, s_pair, r_pair, s_all, r_all,
           s_row, r_row, s_full, r_full, s_last, r_last, s_lown, r_lown):
    r, c, l = lax.axis_index("row"), lax.axis_index("col"), lax.axis_index("layer")
    y, z, xh = r // 4, c // 2, c % 2
    x = r % 4
    mine = (y + x) % 4
    my_core, my_sub = mine // 2, mine % 2

    loads = [
        pltpu.make_async_copy(h_hbm.at[pl.ds(256 * i, 256)], h.at[pl.ds(256 * i, 256)], h_sem.at[i])
        for i in range(4)
    ]
    load_start = pltpu.make_async_copy(start_hbm, start, start_sem)
    load_start.start()
    for load in loads:
        load.start()

    def send(src, dst, s_sem, r_sem, row, col, layer):
        pltpu.make_async_remote_copy(
            src_ref=src, dst_ref=dst, send_sem=s_sem, recv_sem=r_sem,
            device_id=(row, col, layer), device_id_type=MESH,
        ).start()

    def wait(ref, sem):
        pltpu.make_async_copy(ref, ref, sem).wait()

    def each(n, body):
        def step(i, carry):
            body(i)
            return carry

        lax.fori_loop(0, n, step, 0)

    def ring_other(me, i):
        return (me + 4 + (1 - 2 * (i % 2)) * ((i + 1) // 2)) % 8

    def each_ring(me, body):
        each(7, lambda i: body(ring_other(me, i)))

    def each_row(body):
        each(28, lambda i: body(4 * ring_other(y, i // 4) + (x + 2 + i) % 4))
        each(3, lambda i: body(4 * y + (x + 1 + (i + 1) % 3) % 4))

    barrier = pltpu.get_barrier_semaphore()

    def greet(row, col, layer):
        pl.semaphore_signal(barrier, inc=1, device_id=(row, col, layer), device_id_type=MESH)

    def greet_row(other):
        greet(other, c, l)
        greet(other, c, 1 - l)

    each_row(greet_row)
    each_ring(z, lambda other: greet(r, 2 * other + xh, l))
    greet(r, c, 1 - l)
    greet(r, 2 * z + 1 - xh, l)
    load_start.wait()
    for a in range(2):
        startsend[a] = start[...].astype(F32)[4 * a:4 * a + 4].astype(BF16)
    pl.semaphore_wait(barrier, 71)

    for a in range(2):
        landing = raw.at[2 * a + my_sub, y, :, ds(l * 1024, 1024)]
        each_row(lambda other: send(
            startsend.at[a], landing, s_start.at[a], r_start.at[2 * a + my_sub], other, c, my_core))

        @pl.when(l == my_core)
        def _():
            raw[2 * a + my_sub, y, :, ds(l * 1024, 1024)] = startsend[a]

        @pl.when(l != my_core)
        def _():
            send(startsend.at[a], landing, s_own.at[a], r_own.at[a], r, c, my_core)

    low, high = low_ref[0], high_ref[0]
    centre = (low + high) * 0.5
    half_width = (high - low) * 0.5
    scale = 1.0 / half_width
    diag = [
        jnp.where((r // 2 == c) & (r % 2 == half), centre, 0.0) for half in range(2)
    ]

    for load in loads:
        load.wait()

    def take_start(k):
        own = 2 * l + k % 2 == mine

        @pl.when(own)
        def _():
            wait(raw.at[k, pl.ds(0, 7)], r_start.at[k])

            @pl.when(l == my_core)
            def _():
                wait(raw.at[k, y, :, ds((1 - l) * 1024, 1024)], r_own.at[k // 2])

        @pl.when(jnp.logical_not(own))
        def _():
            wait(raw.at[k], r_start.at[k])

        for i in range(2):
            rows = jnp.concatenate([raw[k, 4 * i + j].astype(F32) for j in range(4)], axis=0)
            panel0[k, 16 * i:16 * i + 16, :] = rows.astype(BF16)

    def by_columns(s, k, panel):
        for n in range(4):
            cols = slice(256 * n, 256 * n + 256)
            value = lax.dot_general(
                panel[k], h[cols, :], (((1,), (1,)), ((), ())), preferred_element_type=F32
            )
            for half in range(2):
                lo = 1024 * half + 256 * n
                value = value - diag[half] * panel[k, :, lo:lo + 256].astype(F32)
            colsend[s, k, :, cols] = value.astype(BF16)

        def to(other):
            send(colsend.at[s, k, ds(16 * (other // 4), 16), ds(256 * (other % 4), 256)],
                 colrecv.at[s, k, z], s_cut.at[s, k], r_cut.at[s, k], r, 2 * other + xh, l)

        each_ring(z, to)
        colrecv[s, k, z] = colsend[s, k, ds(16 * (z // 4), 16), ds(256 * (z % 4), 256)]

    def pair_up(s, k):
        wait(colrecv.at[s, k, pl.ds(0, 7)], r_cut.at[s, k])
        total = colrecv[s, k, 0].astype(F32)
        for i in range(1, 8):
            total = total + colrecv[s, k, i].astype(F32)
        colsum[s, k] = total
        pairsend[s, k] = total.astype(BF16)
        send(pairsend.at[s, k], pairrecv.at[s, k], s_pair.at[s, k], r_pair.at[s, k], r, 2 * z + 1 - xh, l)

    def spread_first(s, k):
        wait(pairrecv.at[s, k], r_pair.at[s, k])
        total = colsum[s, k] + pairrecv[s, k].astype(F32)
        rows, cols = ds(16 * (z // 4), 16), ds(256 * (z % 4), 256)
        if s == 0:
            value = scale * total
        else:
            value = 2.0 * scale * total - panel1[0, k, rows, cols].astype(F32)
        panel1[s, k, rows, cols] = value.astype(BF16)
        piece = panel1.at[s, k, rows, cols]
        each_ring(z, lambda other: send(piece, piece, s_all.at[s, k], r_all.at[s, k], r, 2 * other + xh, l))

    def by_rows(s, k):
        wait(colrecv.at[s, k, pl.ds(0, 7)], r_all.at[s, k])
        own = 2 * l + k % 2 == mine
        for n in range(8):
            cols = slice(256 * n, 256 * n + 256)
            lo = (256 * n) % 1024
            value = jnp.dot(panel1[s, k], h[:, cols], preferred_element_type=F32)
            value = value - diag[n // 4] * panel1[s, k, :, lo:lo + 256].astype(F32)
            if s == 0:
                rowsend[k, :, cols] = value.astype(BF16)
            else:
                second = panel2[k, :, cols].astype(F32)
                holds = own & (lax.broadcasted_iota(jnp.int32, value.shape, 0) // 4 == y)
                value = value - jnp.where(holds, half_width * 0.5, 0.0) * second
                for i in range(8):
                    lastsend[k, i, :, cols] = value[4 * i:4 * i + 4].astype(BF16)

    def cut_rows(k):
        def to(other):
            send(rowsend.at[k, ds(16 * (other // 16), 16), ds(128 * (other % 16), 128)],
                 rowrecv.at[k, r], s_row.at[k], r_row.at[k], other, c, l)

        each_row(to)
        rowrecv[k, r] = rowsend[k, ds(16 * (r // 16), 16), ds(128 * (r % 16), 128)]

    def spread_second(k):
        wait(rowrecv.at[k, pl.ds(0, 31)], r_row.at[k])
        total = rowrecv[k, 0].astype(F32)
        for i in range(1, 32):
            total = total + rowrecv[k, i].astype(F32)
        rows, cols = ds(16 * (r // 16), 16), ds(128 * (r % 16), 128)
        value = 2.0 * scale * total - panel0[k, rows, cols].astype(F32)
        panel2[k, rows, cols] = value.astype(BF16)
        piece = panel2.at[k, rows, cols]
        each_row(lambda other: send(piece, piece, s_full.at[k], r_full.at[k], other, c, l))

    def send_last(k):
        own = 2 * l + k % 2 == mine

        def to(i):
            py = ring_other(y, i)
            other = 4 * py + (2 * l + k % 2 + 8 - py) % 4

            @pl.when(other != r)
            def _():
                for half in range(2):
                    send(lastsend.at[k, py, :, pl.ds(1024 * half, 1024)], lastrecv.at[k // 2, r],
                         s_last.at[k], r_last.at[k // 2], other, c, half)

        each(8, to)

        @pl.when(own)
        def _():
            lastrecv[k // 2, r] = lastsend[k, y, :, ds(1024 * l, 1024)]
            send(lastsend.at[k, y, :, ds(1024 * (1 - l), 1024)], lastrecv.at[k // 2, r],
                 s_lown.at[k // 2], r_lown.at[k // 2], r, c, 1 - l)

    def begin(k):
        take_start(k)
        by_columns(0, k, panel0)

    each(CHAINS, begin)
    each(CHAINS, lambda k: pair_up(0, k))
    each(CHAINS, lambda k: spread_first(0, k))

    def middle(k):
        by_rows(0, k)
        cut_rows(k)

    each(CHAINS, middle)
    each(CHAINS, spread_second)

    def again(k):
        wait(rowrecv.at[k, pl.ds(0, 31)], r_full.at[k])
        by_columns(1, k, panel2)

    each(CHAINS, again)
    each(CHAINS, lambda k: pair_up(1, k))
    each(CHAINS, lambda k: spread_first(1, k))

    def finish(k):
        by_rows(1, k)
        send_last(k)

    each(CHAINS, finish)

    parts = []
    for a in range(2):
        wait(lastrecv.at[a, pl.ds(0, 31)], r_last.at[a])

        @pl.when(l != my_core)
        def _():
            wait(lastrecv.at[a, 31], r_lown.at[a])

        total = lastrecv[a, 0].astype(F32)
        for i in range(1, 32):
            total = total + lastrecv[a, i].astype(F32)
        parts.append(2.0 * scale * total)
    out_ref[...] = jnp.concatenate(parts, axis=0).astype(BF16)

    for a in range(2):
        wait(lastrecv.at[a, pl.ds(0, 31)], s_start.at[a])

        @pl.when(l != my_core)
        def _():
            wait(startsend.at[a], s_own.at[a])

        @pl.when(l == my_core)
        def _():
            wait(lastrecv.at[a, 31], s_lown.at[a])

    def drain(k):
        for s in range(2):
            wait(colrecv.at[s, k, pl.ds(0, 7)], s_cut.at[s, k])
            wait(pairsend.at[s, k], s_pair.at[s, k])
            wait(colrecv.at[s, k, pl.ds(0, 7)], s_all.at[s, k])
        wait(rowrecv.at[k, pl.ds(0, 31)], s_row.at[k])
        wait(rowrecv.at[k, pl.ds(0, 31)], s_full.at[k])
        own = 2 * l + k % 2 == mine

        @pl.when(own)
        def _():
            wait(lastsend.at[k, pl.ds(0, 7)], s_last.at[k])

        @pl.when(jnp.logical_not(own))
        def _():
            wait(lastsend.at[k], s_last.at[k])

    each(CHAINS, drain)


def local(hamiltonian, start_vectors, cut_low, cut_high):
    vmem, dma = pltpu.VMEM, pltpu.SemaphoreType.DMA
    n = CHAINS
    return pl.pallas_call(
        kernel,
        out_shape=jax.ShapeDtypeStruct(start_vectors.shape, BF16),
        in_specs=[
            pl.BlockSpec(memory_space=pltpu.SMEM),
            pl.BlockSpec(memory_space=pltpu.SMEM),
            pl.BlockSpec(memory_space=pltpu.HBM),
            pl.BlockSpec(memory_space=pltpu.HBM),
        ],
        out_specs=pl.BlockSpec(memory_space=pltpu.VMEM),
        scratch_shapes=[
            vmem((1024, 2048), BF16),
            vmem((8, 1024), BF16),
            vmem((2, 4, 1024), BF16),
            vmem((n, 8, 4, 2048), BF16),
            vmem((n, 32, 2048), BF16),
            vmem((2, n, 32, 1024), BF16),
            vmem((2, n, 8, 16, 256), BF16),
            vmem((2, n, 16, 256), F32),
            vmem((2, n, 16, 256), BF16),
            vmem((2, n, 16, 256), BF16),
            vmem((2, n, 32, 1024), BF16),
            vmem((n, 32, 2048), BF16),
            vmem((n, 32, 16, 128), BF16),
            vmem((n, 32, 2048), BF16),
            vmem((n, 8, 4, 2048), BF16),
            vmem((2, 32, 4, 1024), BF16),
            dma((4,)), dma,
            dma((2,)), dma((n,)), dma((2,)), dma((2,)),
            dma((2, n)), dma((2, n)), dma((2, n)), dma((2, n)), dma((2, n)), dma((2, n)),
            dma((n,)), dma((n,)), dma((n,)), dma((n,)),
            dma((n,)), dma((2,)), dma((2,)), dma((2,)),
        ],
        compiler_params=pltpu.CompilerParams(
            collective_id=0, has_side_effects=True, vmem_limit_bytes=67_043_328
        ),
        name="filter",
    )(cut_low, cut_high, hamiltonian, start_vectors)


def solution(mesh):
    return jax.shard_map(
        local,
        mesh=mesh,
        in_specs=(P("row", "col"), P("row", ("col", "layer")), P(), P()),
        out_specs=P("row", ("col", "layer")),
        check_vma=False,
    )
```

time: 119 us -> 108 us (0.908); the launches traced: 118 us -> 108 us
  Pallas kernels: 113 us -> 105 us
  local copies, waits for them, and re-layouts: 3.51 us -> 1.32 us
    pallas_call x1, Pallas kernels: 113 us -> 105 us  [local(): pl.pallas_call(kernel, out_shape=jax.ShapeDtypeStruct(start_vectors.shape...]
    unnamed x5 -> x1, local copies, waits for them, and re-layouts: 3.51 us -> 1.32 us
where the time goes in v2:
time: 108 us
  Pallas kernels  105 us (97%)
  local copies, waits for them, and re-layouts  1.32 us (1%)
  between operations  1.3 us (1%)
    pallas_call x1, Pallas kernels, local(): pl.pallas_call(kernel, out_shape=jax.ShapeDtypeStruct(start_vectors.shape...  105 us

profile of v2, /device:TPU:1, one launch (start us, length us, event | category | flops | bytes accessed | tf_op | source)
XLA Modules:
  0.0 108.1 jit_solution(13548005139967830092)
XLA Ops:
  1.3 105.4 %filter.1 = bf16[8,1024]{1,0:T(8,128)(2,1)} custom-call(f32[1]{0:T(128)S(6)} %copy.6.low_ref, f32[1]{0:T(128)S(6)} %copy.7.high_ref, bf16[1024,2048]{1,0:T(8,128)(2,1)} %h_hbm.1, bf16[8,1024]{1,0:T(8,128)(2,1)} %start_hbm.1), custom_call_target="tpu_custom_call" | custom-call | tf_op jit(solution)/shard_map/filter/pallas_call | solution.py:299
  106.7 1.3 %copy.8 = bf16[8,1024]{1,0:T(8,128)(2,1)} copy(bf16[8,1024]{1,0:T(8,128)(2,1)} %filter.1) | data formatting | bytes 32768
